TPU v7x, 256 devices: a whole 4x4x8 slice. The times are simulated.
256 devices in a mesh: space: 4 (over z_hi, core), fsdp: 64 (over y, x, z_lo).
Axes of the slice: x: 4, y: 4, z: 8 (z_hi: 2, z_lo: 4; z = z_hi * 4 + z_lo), core: 2. Of those that a mesh axis runs over, the one named last changes fastest.
Arguments:
- acts: bfloat16 [64, 8, 16, 16, 512], P('fsdp', 'space'), may hold values from -16 to 16
- kernel: bfloat16 [512, 27, 256], P('fsdp'), may hold values from -0.0546875 to 0.0546875
- cotangent: bfloat16 [64, 8, 16, 16, 256], P('fsdp', 'space'), may hold values from -6 to 6
Outputs:
- outputs: bfloat16 [64, 8, 16, 16, 256], P('fsdp', 'space')
- grad_input: bfloat16 [64, 8, 16, 16, 512], P('fsdp', 'space')
- grad_kernel: float32 [512, 27, 256], P('fsdp')
All inputs are finite; a program needn't handle non-finite values.
Results may differ from a plain program's by a relative error of at most 0.0095.
Values may be sent and summed in bfloat16 or wider, within the bound.
A program may use at most 128 MiB of HBM per device.

v0:
```python
import jax
import jax.numpy as jnp
from jax import lax
from jax.sharding import PartitionSpec as P

kernel_offsets = [(i // 9 - 1, i // 3 % 3 - 1, i % 3 - 1) for i in range(27)]


def padded(block, sides, width):
    for axis, dim in sides:
        count = lax.axis_size(axis)
        forward = [(i, i + 1) for i in range(count - 1)]
        backward = [(target, source) for source, target in forward]
        low = lax.ppermute(
            lax.slice_in_dim(block, block.shape[dim] - width, None, axis=dim), axis, forward
        )
        high = lax.ppermute(lax.slice_in_dim(block, 0, width, axis=dim), axis, backward)
        block = jnp.concatenate([low, block, high], axis=dim)
    return block


def from_everyone(x, axis):
    copies = jnp.broadcast_to(x, (lax.axis_size(axis), *x.shape))
    return lax.all_to_all(copies, axis, split_axis=0, concat_axis=0, tiled=True)


def of_everyone(x, axis):
    everything = from_everyone(x, axis)
    return jnp.sum(everything.astype(jnp.float32), axis=0)


def body(acts, kernel, cotangent):
    local_acts = acts[0]
    local_grad = cotangent[0]
    slab_len = local_acts.shape[0]
    side_len = local_acts.shape[1]
    chan_in = local_acts.shape[3]
    chan_out = local_grad.shape[3]
    tap_count = len(kernel_offsets)
    padded_side = side_len + 2
    plane = padded_side * padded_side
    margin = padded_side + 1
    grid_rows = slab_len * plane
    centre = margin + plane
    acts_float = local_acts.astype(jnp.float32)
    squash = jax.nn.sigmoid(acts_float)
    hidden = (acts_float * squash).astype(jnp.bfloat16)
    joined = jnp.concatenate([hidden, local_grad], axis=3)[None]
    framed = padded(joined, (("space", 1),), 1)[0]
    framed = jnp.pad(framed, ((0, 0), (1, 1), (1, 1), (0, 0)))
    flat_all = framed.reshape((slab_len + 2) * plane, chan_in + chan_out)
    flat_all = jnp.pad(flat_all, ((margin, margin), (0, 0)))
    hidden_flat = flat_all[:, :chan_in]
    grad_flat_pad = flat_all[:, chan_in:]
    grad_centre = grad_flat_pad[centre : centre + grid_rows]

    def offset_of(tap_index):
        shift_d, shift_h, shift_w = kernel_offsets[tap_index]
        return shift_d * plane + shift_h * padded_side + shift_w

    empty_out = jnp.zeros((grid_rows, chan_out), jnp.float32)
    running = empty_out
    shard_rows = lax.all_gather(kernel, "fsdp", axis=0, tiled=True)
    channel_part = hidden_flat
    for tap_index in range(tap_count):
        begin = centre + offset_of(tap_index)
        running = running + jnp.dot(
            channel_part[begin : begin + grid_rows],
            shard_rows[:, tap_index, :],
            preferred_element_type=jnp.float32,
        )
    shard_rows = lax.all_gather(kernel, "fsdp", axis=0, tiled=True)
    row_count = shard_rows.shape[0]
    total = jnp.zeros((grid_rows, row_count), jnp.float32)
    for tap_index in range(tap_count):
        begin = centre - offset_of(tap_index)
        total = total + lax.dot_general(
            grad_flat_pad[begin : begin + grid_rows],
            shard_rows[:, tap_index, :],
            (((1,), (1,)), ((), ())),
            preferred_element_type=jnp.float32,
        )
    back = total.reshape(1, slab_len, padded_side, padded_side, row_count)
    back_inner = back[0][:, 1:-1, 1:-1, :]
    grad_input = (back_inner * squash * (1.0 + acts_float * (1.0 - squash))).astype(jnp.bfloat16)[
        None
    ]
    batch_scale = 1.0 / lax.axis_size("fsdp")
    channel_part = hidden_flat
    pieces = []
    for tap_index in range(tap_count):
        begin = centre + offset_of(tap_index)
        pieces.append(
            lax.dot_general(
                channel_part[begin : begin + grid_rows],
                grad_centre,
                (((0,), (0,)), ((), ())),
                preferred_element_type=jnp.float32,
            )
        )
    term = jnp.concatenate(pieces, axis=1)
    owned_share = lax.psum_scatter(
        term.reshape(kernel.shape[0] * lax.axis_size("fsdp"), tap_count, chan_out) * batch_scale,
        "fsdp",
        scatter_dimension=0,
        tiled=True,
    )
    grad_kernel = of_everyone(owned_share.astype(jnp.bfloat16), "space").astype(jnp.float32)
    shaped = running.reshape(slab_len, padded_side, padded_side, running.shape[-1])
    outputs = shaped[:, 1:-1, 1:-1, :].astype(jnp.bfloat16)[None]
    return (outputs, grad_input, grad_kernel)


def solution(mesh):
    return jax.shard_map(
        body,
        mesh=mesh,
        in_specs=(
            P("fsdp", "space", None, None, None),
            P("fsdp", None, None),
            P("fsdp", "space", None, None, None),
        ),
        out_specs=(
            P("fsdp", "space", None, None, None),
            P("fsdp", "space", None, None, None),
            P("fsdp", None, None),
        ),
        check_vma=False,
    )
```

profile of v0, /device:TPU:3, one launch (start us, length us, event | category | flops | bytes accessed | tf_op | source)
XLA Modules:
  0.0 794.8 jit_solution(10638212462257670923)
XLA Ops:
  7.9 1.4 fusion.4
  10.4 9.4 %collective-permute-start = (bf16[1,1,16,16,768]{4,3,2,1,0:T(8,128)(2,1)S(1)}, bf16[1,1,16,16,768]{4,3,2,1,0:T(8,128)(2,1)S(1)}, u32[]{:S(2)}, u32[]{:S(2)}) collective-permute-start(bf16[1,1,16,16,768]{4,3,2,1,0:T(8,128)(2,1)S(1)} %get-tuple-element.3), channel_id=1, source_target_pairs={{0,64},{64,128},{128,192},{1,65},{65,129},{129,193},{2,66},{66,130... | collective-permute-start | bytes 1179656 | tf_op jit(solution)/shard_map/ppermute | solution.py:14
  19.8 1.9 collective-permute-start.1
  21.7 3.5 collective-permute-done
  25.2 15.5 %collective-permute-done.1 = bf16[1,1,16,16,768]{4,3,2,1,0:T(8,128)(2,1)S(1)} collective-permute-done((bf16[1,1,16,16,768]{4,3,2,1,0:T(8,128)(2,1)S(1)}, bf16[1,1,16,16,768]{4,3,2,1,0:T(8,128)(2,1)S(1)}, u32[]{:S(2)}, u32[]{:S(2)}) %collective-permute-start.1) | collective-permute-done | bytes 393248 | tf_op jit(solution)/shard_map/ppermute | solution.py:17
  40.9 2.6 pad.8
  43.6 2.9 reshape.18
  65.2 1.3 convolution_dynamic-update-slice_fusion.11
  66.5 1.3 convolution_dynamic-update-slice_fusion.10
  67.8 1.3 convolution_dynamic-update-slice_fusion.9
  80.3 12.1 %broadcast_multiply_fusion = f32[512,6912]{0,1:T(8,128)} fusion(f32[512,6912]{0,1:T(8,128)} %convolution_dynamic-update-slice_fusion), kind=kLoop, calls=%fused_computation | loop fusion | flops 3538944 | bytes 28311552 | tf_op jit(solution)/shard_map/mul | solution.py:103
  92.4 19.9 %copy.10 = f32[512,27,256]{2,1,0:T(8,128)} copy(f32[512,27,256]{0,2,1:T(8,128)} %bitcast.124) | data formatting | bytes 28311552 | tf_op jit(solution)/shard_map/mul | solution.py:103
  112.4 188.4 %all-gather.2.cloned.1.call-done = bf16[512,27,256]{2,0,1:T(8,128)(2,1)} async-done(((bf16[8,27,256]{2,0,1:T(8,128)(2,1)}), bf16[512,27,256]{2,0,1:T(8,128)(2,1)}) %all-gather.2.cloned.1.call-update) | async-done | bytes 7077904 | tf_op jit(solution)/shard_map/all_gather | solution.py:63
  300.7 1.3 fusion.61
  302.1 1.5 fusion.89
  303.5 1.7 convolution_add_fusion.51
  325.0 396.1 %reduce-scatter.2.cloned.1.call-done = f32[8,27,256]{2,1,0:T(8,128)} async-done(((f32[512,27,256]{2,1,0:T(8,128)}), f32[8,27,256]{2,1,0:T(8,128)}) %reduce-scatter.2.cloned.1.call-update) | async-done | bytes 221200 | tf_op jit(solution)/shard_map/reduce_scatter | solution.py:102
  723.0 52.2 %all-to-all-start = ((bf16[4,8,27,256]{3,1,2,0:T(8,128)(2,1)}), bf16[4,8,27,256]{3,1,2,0:T(8,128)(2,1)}, u32[]{:S(2)}, u32[]{:S(2)}) async-start(bf16[4,8,27,256]{3,1,2,0:T(8,128)(2,1)} %broadcast_in_dim.15), calls=%async_computation.1 | async-start | bytes 884736 | tf_op jit(solution)/shard_map/all_to_all | solution.py:24
  775.2 2.2 fusion
  777.4 1.8 reshape.19
  779.5 1.8 slice_bitcast_fusion
  781.3 2.3 fusion.63
  783.5 2.6 all-to-all-done
  786.2 1.8 convert_reduce_fusion
  (86 shorter events, 53.4 us)
Async XLA Ops:
  7.2 293.6 %all-gather.2.cloned.1.call-start = ((), (), s32[]{:S(2)}) async-start(), calls=%async_computation.2 | async-start | bytes 7188480 | tf_op jit(solution)/shard_map/all_gather | solution.py:63
  7.9 713.2 %reduce-scatter.2.cloned.1.call-start = ((), (), s32[]{:S(2)}) async-start(), calls=%async_computation.3 | async-start | bytes 17039360 | tf_op jit(solution)/shard_map/reduce_scatter | solution.py:102
  10.4 14.8 %collective-permute-start = (bf16[1,1,16,16,768]{4,3,2,1,0:T(8,128)(2,1)S(1)}, bf16[1,1,16,16,768]{4,3,2,1,0:T(8,128)(2,1)S(1)}, u32[]{:S(2)}, u32[]{:S(2)}) collective-permute-start(bf16[1,1,16,16,768]{4,3,2,1,0:T(8,128)(2,1)S(1)} %get-tuple-element.3), channel_id=1, source_target_pairs={{0,64},{64,128},{128,192},{1,65},{65,129},{129,193},{2,66},{66,130... | collective-permute-start | bytes 1179656 | tf_op jit(solution)/shard_map/ppermute | solution.py:14
  19.8 21.0 %collective-permute-start.1 = (bf16[1,1,16,16,768]{4,3,2,1,0:T(8,128)(2,1)S(1)}, bf16[1,1,16,16,768]{4,3,2,1,0:T(8,128)(2,1)S(1)}, u32[]{:S(2)}, u32[]{:S(2)}) collective-permute-start(bf16[1,1,16,16,768]{4,3,2,1,0:T(8,128)(2,1)S(1)} %get-tuple-element.4), channel_id=1, source_target_pairs={{64,0},{128,64},{192,128},{65,1},{129,65},{193,129},{66,2},{130,66... | collective-permute-start | bytes 1179656 | tf_op jit(solution)/shard_map/ppermute | solution.py:17
  302.0 3.2 copy-start
  723.0 63.2 %all-to-all-start = ((bf16[4,8,27,256]{3,1,2,0:T(8,128)(2,1)}), bf16[4,8,27,256]{3,1,2,0:T(8,128)(2,1)}, u32[]{:S(2)}, u32[]{:S(2)}) async-start(bf16[4,8,27,256]{3,1,2,0:T(8,128)(2,1)} %broadcast_in_dim.15), calls=%async_computation.1 | async-start | bytes 884736 | tf_op jit(solution)/shard_map/all_to_all | solution.py:24
Sparse Core Ops, SparseCore 0:
  9.7 291.0 all-gather.1
  303.3 417.7 reduce-scatter.1
where the time goes:
time: 808 us; the launch traced here: 795 us
  waiting for transfers between devices  607 us (75%)
  starting transfers between devices  63.6 us (8%)
  matrix products  59.8 us (7%)
  local copies, waits for them, and re-layouts  31.2 us (4%)
  other arithmetic  18.7 us (2%)
  between operations  14.5 us (2%)
    reduce_scatter x1, waiting for transfers between devices, body(): lax.psum_scatter(term.reshape(kernel.shape[0] * lax.axis_size('fsdp'), ta...  396 us
    all_gather x1, waiting for transfers between devices, body(): shard_rows = lax.all_gather(kernel, 'fsdp', axis=0, tiled=True)  188 us
    all_to_all x1, starting transfers between devices, from_everyone(): return lax.all_to_all(copies, axis, split_axis=0, concat_axis=0, tiled=True)  52.2 us
    dot_general x27, matrix products, body(): lax.dot_general(channel_part[begin:begin + grid_rows], grad_centre, (((0,...  33.8 us
    mul x1, local copies, waits for them, and re-layouts, body(): term.reshape(kernel.shape[0] * lax.axis_size('fsdp'), tap_count, chan_out)  19.9 us
  transfers between devices with their start and end apart: 5, of which 5 were waited for; matrix products, arithmetic and copies ran while one was open for 13% of the time, Pallas kernels for 0%

commit v1 on v0

v1 whole, which is shorter than its diff:
```python
import functools

import jax
import jax.numpy as jnp
from jax import lax
from jax.experimental import pallas as pl
from jax.experimental.pallas import tpu as pltpu
from jax.sharding import PartitionSpec as P

MESH = pl.DeviceIdType.MESH
F32 = jnp.float32
BF16 = jnp.bfloat16
ORDERS = (("z", "x", "y"), ("y", "z", "x"), ("x", "y", "z"))
LOW, HIGH = pl.ds(0, 2), pl.ds(2, 2)
COPIES = 128


def silu(v):
    return v * jax.nn.sigmoid(v)


def step_kernel(
    acts,
    cot,
    shard,
    outputs,
    grad_input,
    grad_kernel,
    weights,
    partial,
    from_partner,
    rx3p,
    rx3m,
    rx2p,
    rx2m,
    rx1,
    own_sum,
    other_sum,
    final_own,
    final_other,
    hidden3,
    cot3,
    hidden_t,
    halo_acts,
    halo_cot,
    acc_out,
    acc_back,
    send_sem,
    recv_sem,
    local_sem,
):
    space, fsdp = lax.axis_index("space"), lax.axis_index("fsdp")
    core, z_hi = space % 2, space // 2
    y, x, zl = fsdp // 16, (fsdp // 4) % 4, fsdp % 4
    z = z_hi * 4 + zl
    own = {"y": y, "x": x, "z": zl}

    def neighbour(dim, delta):
        if dim == "y":
            return (space, ((y + 4 + delta) % 4) * 16 + x * 4 + zl)
        if dim == "x":
            return (space, y * 16 + ((x + 4 + delta) % 4) * 4 + zl)
        there = (z + 8 + delta) % 8
        return ((there // 4) * 2 + core, y * 16 + x * 4 + there % 4)

    partner = (z_hi * 2 + 1 - core, fsdp)
    across = ((space + 2) % 4, fsdp)
    greeted = [neighbour(d, k) for d in ("y", "x") for k in (1, -1, 2)]
    greeted += [neighbour("z", k) for k in (1, -1, 2, -2)]
    greeted += [partner, across, (3 - space, fsdp)]

    barrier = pltpu.get_barrier_semaphore()
    for device in greeted:
        pl.semaphore_signal(barrier, inc=1, device_id=device, device_id_type=MESH)
    pl.semaphore_wait(barrier, len(greeted))

    counter = [0]
    sent = []

    def remote(src, dst, device):
        number = counter[0]
        counter[0] += 1
        return pltpu.make_async_remote_copy(
            src_ref=src,
            dst_ref=dst,
            send_sem=send_sem.at[number],
            recv_sem=recv_sem.at[number],
            device_id=device,
            device_id_type=MESH,
        )

    def send(src, dst, device):
        copy = remote(src, dst, device)
        copy.start()
        sent.append(copy)
        return copy

    def at(dim, delta):
        return (own[dim] + 4 + delta) % 4

    def place(colour, first, second, third):
        d1, d2, d3 = ORDERS[colour]
        index = {d1: first, d2: second, d3: third}
        return index["y"], index["x"], index["z"]

    every = slice(None)

    halo_copies = []
    for src, dst in ((cot, halo_cot), (acts, halo_acts)):
        down = remote(src.at[0], dst.at[1], (space - 1, fsdp))
        up = remote(src.at[1], dst.at[0], (space + 1, fsdp))
        halo_copies.append((down, up))

    def each_halo(number, action_down, action_up):
        down, up = halo_copies[number]

        @pl.when(space > 0)
        def _():
            action_down(down, up)

        @pl.when(space < 3)
        def _():
            action_up(down, up)

    def start_halo(number):
        each_halo(number, lambda d, u: d.start(), lambda d, u: u.start())

    def take_halo(number):
        each_halo(number, lambda d, u: u.wait_recv(), lambda d, u: d.wait_recv())

    def end_halo(number):
        each_halo(number, lambda d, u: d.wait_send(), lambda d, u: u.wait_send())

    def slot(colour, first, second, third):
        iy, ix, iz = place(colour, first, second, third)
        return weights.at[core, pl.ds(9 * colour, 9), iy, ix, iz]

    waiting = {}

    def spread(key, colour, where, device):
        piece = slot(colour, *where)
        waiting.setdefault(key, []).append(send(piece, piece, device))

    def take(key):
        for copy in waiting.pop(key):
            copy.wait_recv()

    def gather_0():
        for colour, (d1, d2, d3) in enumerate(ORDERS):
            here = slot(colour, own[d1], own[d2], own[d3])
            for delta in (1, -1, 2):
                copy = send(shard.at[core, pl.ds(9 * colour, 9)], here, neighbour(d1, delta))
                waiting.setdefault("a1", []).append(copy)

    def gather_1():
        take("a1")
        for colour, (d1, d2, d3) in enumerate(ORDERS):
            for delta in (1, -1):
                spread("a2", colour, (every, own[d2], own[d3]), neighbour(d2, delta))

    def gather_2():
        take("a2")
        for colour, (d1, d2, d3) in enumerate(ORDERS):
            spread("a3", colour, (LOW, at(d2, -1), own[d3]), neighbour(d2, 1))
            spread("a3", colour, (HIGH, at(d2, 1), own[d3]), neighbour(d2, -1))

    def gather_3():
        take("a3")
        for colour, (d1, d2, d3) in enumerate(ORDERS):
            for delta in (1, -1):
                spread("a4", colour, (every, every, own[d3]), neighbour(d3, delta))
        for colour, (d1, d2, d3) in enumerate(ORDERS):
            spread("pair", colour, (every, every, own[d3]), partner)

    def gather_4():
        take("a4")
        for colour, (d1, d2, d3) in enumerate(ORDERS):
            spread("a5", colour, (LOW, every, at(d3, -1)), neighbour(d3, 1))
            spread("a5", colour, (HIGH, every, at(d3, 1)), neighbour(d3, -1))
        for colour, (d1, d2, d3) in enumerate(ORDERS):
            for delta in (1, -1):
                spread("pair", colour, (every, every, at(d3, delta)), partner)

    def gather_5():
        take("a5")
        for colour, (d1, d2, d3) in enumerate(ORDERS):
            spread("pair", colour, (LOW, every, at(d3, 2)), partner)
            spread("pair", colour, (HIGH, every, at(d3, 2)), partner)

    def gather_6():
        take("pair")

    def term(ref, colour, first, second, third, taps=None):
        iy, ix, iz = place(colour, first, second, third)
        taps = pl.ds(9 * colour, 9) if taps is None else taps
        if ref is partial:
            return (core, taps, iy, ix, iz)
        return (taps, iy, ix, iz)

    def pass_on(key, colour, where, dst, device):
        src = partial.at[term(partial, colour, *where)]
        copy = send(src, dst.at[term(dst, colour, *where)], device)
        waiting.setdefault(key, []).append(copy)

    def add(colour, where, *others):
        def one(tap, carry):
            tap = tap + 9 * colour
            mine = term(partial, colour, *where, taps=tap)
            total = partial[mine].astype(F32)
            for ref in others:
                total = total + ref[term(ref, colour, *where, taps=tap)].astype(F32)
            partial[mine] = total.astype(BF16)
            return carry

        lax.fori_loop(0, 9, one, 0)

    def reduce_pair(colour):
        taps = pl.ds(9 * colour, 9)
        copy = send(partial.at[1 - core, taps], from_partner.at[taps], partner)
        waiting.setdefault(f"p{colour}", []).append(copy)

    def reduce_phase(phase, part):
        plus, minus = (rx3p, rx3m) if phase == 3 else (rx2p, rx2m)
        for colour, order in enumerate(ORDERS):
            dim = order[phase - 1]

            def where(half, delta):
                if phase == 3:
                    return (half, every, at(dim, delta))
                return (half, at(dim, delta), own[order[2]])

            forward, backward = neighbour(dim, 1), neighbour(dim, -1)
            if part == 0:
                key = f"far{phase}{colour}"
                pass_on(key, colour, where(LOW, 2), plus, forward)
                pass_on(key, colour, where(HIGH, 2), minus, backward)
                key = f"near{phase}{colour}"
                pass_on(key, colour, where(HIGH, 1), plus, forward)
                pass_on(key, colour, where(LOW, -1), minus, backward)
            elif part == 1:
                take(f"far{phase}{colour}")
                key = f"near{phase}{colour}"
                add(colour, where(LOW, 1), plus)
                pass_on(key, colour, where(LOW, 1), plus, forward)
                add(colour, where(HIGH, -1), minus)
                pass_on(key, colour, where(HIGH, -1), minus, backward)
            else:
                take(f"near{phase}{colour}")
                add(colour, where(every, 0), plus, minus)

    def reduce_1():
        for colour in range(3):
            take(f"p{colour}")
            add(colour, (every, every, every), from_partner)
        reduce_phase(3, 0)

    def reduce_2():
        reduce_phase(3, 1)

    def reduce_3():
        reduce_phase(3, 2)
        reduce_phase(2, 0)

    def reduce_4():
        reduce_phase(2, 1)

    def reduce_5():
        reduce_phase(2, 2)
        for colour, (d1, d2, d3) in enumerate(ORDERS):
            for number, delta in enumerate((1, -1, 2)):
                src = partial.at[term(partial, colour, at(d1, delta), own[d2], own[d3])]
                dst = rx1.at[number, pl.ds(9 * colour, 9)]
                waiting.setdefault("r6", []).append(send(src, dst, neighbour(d1, delta)))

    def reduce_6():
        take("r6")
        for tap in range(27):
            total = partial[core, tap, y, x, zl].astype(F32)
            for number in range(3):
                total = total + rx1[number, tap].astype(F32)
            own_sum[tap] = total.astype(BF16)
        waiting["r7"] = [send(own_sum, other_sum, across)]

    def reduce_7(scale):
        take("r7")
        final_own[...] = (own_sum[...].astype(F32) + other_sum[...].astype(F32)) * scale
        waiting["r8"] = [send(final_own, final_other, partner)]
        grad_kernel[core] = final_own[...]

    def reduce_8():
        take("r8")
        grad_kernel[1 - core] = final_other[...]

    def shifted(values):
        rows = values.shape[0]
        w = lax.broadcasted_iota(jnp.int32, values.shape, 0) % 16
        before = jnp.where(w == 0, 0.0, pltpu.roll(values, 1, axis=0))
        after = jnp.where(w == 15, 0.0, pltpu.roll(values, rows - 1, axis=0))
        return before.astype(BF16), values.astype(BF16), after.astype(BF16)

    def put_hidden(values, d, h, count):
        for number, part in enumerate(shifted(values)):
            hidden3[number, d, pl.ds(h, count)] = part.reshape(count, 16, 512)

    def put_cot(values, d, h, count):
        for number, part in enumerate(shifted(values)):
            cot3[2 - number, d, pl.ds(h, count)] = part.reshape(count, 16, 256)

    def prepare_cot():
        for ref, width in ((cot3, 256), (hidden3, 512)):
            edge = jnp.zeros((3, 4, 16, width), BF16)
            ref[:, :, 0] = edge
            ref[:, :, 17] = edge

        def one(i, carry):
            d, h = i // 4, (i % 4) * 4
            values = cot[d, pl.ds(h, 4)].astype(F32).reshape(64, 256)
            put_cot(values, d + 1, h + 1, 4)
            return carry

        lax.fori_loop(0, 8, one, 0)

    def prepare_hidden():
        for i in range(4):
            d, h = i // 2, (i % 2) * 8
            values = silu(acts[d, pl.ds(h, 8)].astype(F32).reshape(128, 512))
            put_hidden(values, d + 1, h + 1, 8)
            hidden_t[:, 128 * i : 128 * i + 128] = values.T.astype(BF16)

    def fill_halo(number):
        take_halo(number)
        halo, put, width = (
            (halo_cot, put_cot, 256) if number == 0 else (halo_acts, put_hidden, 512)
        )
        for side, there in ((0, space > 0), (1, space < 3)):

            @pl.when(there)
            def _():
                def one(i, carry):
                    values = halo[side, pl.ds(i * 4, 4)].astype(F32).reshape(64, width)
                    put(silu(values) if number == 1 else values, 3 * side, i * 4 + 1, 4)
                    return carry

                lax.fori_loop(0, 4, one, 0)

            @pl.when(jnp.logical_not(there))
            def _():
                target = cot3 if number == 0 else hidden3
                target[:, 3 * side] = jnp.zeros((3, 18, 16, width), BF16)

    def cot_rows(colour, b, number):
        rows = cot3[number, pl.ds(2 - colour, 2), pl.ds(2 - b, 16)]
        return rows.reshape(512, 256)

    def kernel_term(colour, b):
        def one(number, carry):
            product = jnp.dot(
                hidden_t[...], cot_rows(colour, b, number), preferred_element_type=F32
            )
            tap = 9 * colour + 3 * b + number
            for half in range(2):
                part = product[:, 128 * half : 128 * half + 128]
                partial[half, tap] = part.reshape(4, 4, 4, 8, 128).astype(BF16)
            return carry

        lax.fori_loop(0, 3, one, 0)

    def tap_weight(tap):
        halves = [weights[half, tap].reshape(512, 128) for half in range(2)]
        return jnp.concatenate(halves, axis=1)

    def forward_and_back(colour, b, first):
        taps = [tap_weight(9 * colour + 3 * b + number) for number in range(3)]
        rows = [
            hidden3[number, pl.ds(colour, 2), pl.ds(b, 16)].reshape(512, 512)
            for number in range(3)
        ]
        product = jnp.dot(
            jnp.concatenate(rows, axis=1),
            jnp.concatenate(taps, axis=0),
            preferred_element_type=F32,
        )
        acc_out[...] = product if first else acc_out[...] + product
        grads = [cot_rows(colour, b, number) for number in range(3)]
        product = lax.dot_general(
            jnp.concatenate(grads, axis=1),
            jnp.concatenate(taps, axis=1),
            (((1,), (1,)), ((), ())),
            preferred_element_type=F32,
        )
        acc_back[...] = product if first else acc_back[...] + product

    gather_0()
    start_halo(0)
    start_halo(1)
    mine = pltpu.make_async_copy(shard.at[core], weights.at[core, :, y, x, zl], local_sem)
    mine.start()
    prepare_cot()
    prepare_hidden()
    mine.wait()
    gather_1()
    kernel_term(1, 0)
    kernel_term(1, 1)
    gather_2()
    kernel_term(1, 2)
    reduce_pair(1)
    gather_3()
    fill_halo(0)
    for b in range(3):
        kernel_term(0, b)
    reduce_pair(0)
    kernel_term(2, 0)
    gather_4()
    kernel_term(2, 1)
    kernel_term(2, 2)
    reduce_pair(2)
    reduce_1()
    gather_5()
    fill_halo(1)
    gather_6()
    forward_and_back(1, 0, True)
    forward_and_back(1, 1, False)
    reduce_2()
    forward_and_back(1, 2, False)
    forward_and_back(0, 0, False)
    reduce_3()
    forward_and_back(0, 1, False)
    reduce_4()
    forward_and_back(0, 2, False)
    reduce_5()
    forward_and_back(2, 0, False)
    reduce_6()
    forward_and_back(2, 1, False)
    forward_and_back(2, 2, False)
    reduce_7(1.0 / lax.axis_size("fsdp"))
    outputs[...] = acc_out[...].astype(BF16).reshape(outputs.shape)
    for i in range(8):
        d, h = i // 4, (i % 4) * 4
        values = acts[d, pl.ds(h, 4)].astype(F32).reshape(64, 512)
        squash = jax.nn.sigmoid(values)
        slope = squash * (1.0 + values * (1.0 - squash))
        total = acc_back[64 * i : 64 * i + 64] * slope
        grad_input[d, pl.ds(h, 4)] = total.astype(BF16).reshape(4, 16, 512)
    reduce_8()
    for copy in sent:
        copy.wait_send()
    end_halo(0)
    end_halo(1)


def body(acts, kernel, cotangent):
    shard = kernel.reshape(8, 27, 2, 128).transpose(2, 1, 0, 3)
    vmem = pl.BlockSpec(memory_space=pltpu.VMEM)
    whole = (27, 4, 4, 4, 8, 128)
    outputs, grad_input, grad_kernel = pl.pallas_call(
        step_kernel,
        out_shape=(
            jax.ShapeDtypeStruct((2, 16, 16, 256), BF16),
            jax.ShapeDtypeStruct((2, 16, 16, 512), BF16),
            jax.ShapeDtypeStruct((2, 27, 8, 128), F32),
        ),
        in_specs=[vmem] * 3,
        out_specs=(vmem,) * 3,
        scratch_shapes=[
            pltpu.VMEM((2, *whole), BF16),
            pltpu.VMEM((2, *whole), BF16),
            pltpu.VMEM(whole, BF16),
            pltpu.VMEM(whole, BF16),
            pltpu.VMEM(whole, BF16),
            pltpu.VMEM(whole, BF16),
            pltpu.VMEM(whole, BF16),
            pltpu.VMEM((3, 27, 8, 128), BF16),
            pltpu.VMEM((27, 8, 128), BF16),
            pltpu.VMEM((27, 8, 128), BF16),
            pltpu.VMEM((27, 8, 128), F32),
            pltpu.VMEM((27, 8, 128), F32),
            pltpu.VMEM((3, 4, 18, 16, 512), BF16),
            pltpu.VMEM((3, 4, 18, 16, 256), BF16),
            pltpu.VMEM((512, 512), BF16),
            pltpu.VMEM((2, 16, 16, 512), BF16),
            pltpu.VMEM((2, 16, 16, 256), BF16),
            pltpu.VMEM((512, 256), F32),
            pltpu.VMEM((512, 512), F32),
            pltpu.SemaphoreType.DMA((COPIES,)),
            pltpu.SemaphoreType.DMA((COPIES,)),
            pltpu.SemaphoreType.DMA,
        ],
        compiler_params=pltpu.CompilerParams(
            collective_id=0, has_side_effects=True, vmem_limit_bytes=66_000_000
        ),
        cost_estimate=pl.CostEstimate(
            flops=11_000_000_000, bytes_accessed=4_000_000, transcendentals=1_000_000
        ),
    )(acts[0], cotangent[0], shard)
    grad_kernel = grad_kernel.transpose(2, 1, 0, 3).reshape(8, 27, 256)
    return outputs[None], grad_input[None], grad_kernel


def solution(mesh):
    return jax.shard_map(
        body,
        mesh=mesh,
        in_specs=(
            P("fsdp", "space", None, None, None),
            P("fsdp", None, None),
            P("fsdp", "space", None, None, None),
        ),
        out_specs=(
            P("fsdp", "space", None, None, None),
            P("fsdp", "space", None, None, None),
            P("fsdp", None, None),
        ),
        check_vma=False,
    )
```

time: 808 us -> 82.3 us (0.10); the launches traced: 795 us -> 80.7 us
  waiting for transfers between devices: 607 us -> 0 us
  Pallas kernels: 0 us -> 74.3 us
  starting transfers between devices: 63.6 us -> 0 us
  matrix products: 59.8 us -> 0 us
  local copies, waits for them, and re-layouts: 31.2 us -> 5.71 us
  other arithmetic: 18.7 us -> 0 us
  between operations: 14.5 us -> 0.66 us
    reduce_scatter x1 -> x0, waiting for transfers between devices: 396 us -> none  [body(): lax.psum_scatter(term.reshape(kernel.shape[0] * lax.axis_size('fsdp'), ta...]
    all_gather x1 -> x0, waiting for transfers between devices: 188 us -> none  [body(): shard_rows = lax.all_gather(kernel, 'fsdp', axis=0, tiled=True)]
    pallas_call x0 -> x1, Pallas kernels: none -> 74.3 us  [body(): pl.pallas_call(step_kernel, out_shape=(jax.ShapeDtypeStruct((2, 16, 16, 2...]
    dot_general x81 -> x0, matrix products: 59.8 us -> none  [the longest x27 33.8 us: body(): lax.dot_general(channel_part[begin:begin + grid_rows], grad_centre, (((0,...]
    all_to_all x1 -> x0, starting transfers between devices: 52.2 us -> none  [from_everyone(): return lax.all_to_all(copies, axis, split_axis=0, concat_axis=0, tiled=True)]
    mul x1 -> x0, local copies, waits for them, and re-layouts: 19.9 us -> none  [body(): term.reshape(kernel.shape[0] * lax.axis_size('fsdp'), tap_count, chan_out)]
    ppermute x2 -> x0, waiting for transfers between devices: 19 us -> none  [the longest x1 15.5 us: padded(): lax.ppermute(lax.slice_in_dim(block, 0, width, axis=dim), axis, backward)]
    mul x1 -> x0, other arithmetic: 12.1 us -> none  [body(): term.reshape(kernel.shape[0] * lax.axis_size('fsdp'), tap_count, chan_out)]
  transfers between devices with their start and end apart: 5 -> 0, of which waited for: 5 -> 0; matrix products, arithmetic and copies ran while one was open for 13% -> 0% of each run, Pallas kernels for 0% -> 0%
where the time goes in v1:
time: 82.3 us; the launch traced here: 80.7 us
  Pallas kernels  74.3 us (90%)
  local copies, waits for them, and re-layouts  5.71 us (7%)
    pallas_call x1, Pallas kernels, body(): pl.pallas_call(step_kernel, out_shape=(jax.ShapeDtypeStruct((2, 16, 16, 2...  74.3 us
    unnamed x6, local copies, waits for them, and re-layouts  3.36 us
    reshape x1, local copies, waits for them, and re-layouts, body(): grad_kernel = grad_kernel.transpose(2, 1, 0, 3).reshape(8, 27, 256)  1.69 us

profile of v1, /device:TPU:3, one launch (start us, length us, event | category | flops | bytes accessed | tf_op | source)
XLA Modules:
  0.0 80.7 jit_solution(9299591481833899966)
XLA Ops:
  0.6 0.0 copy-start
  0.6 0.9 %copy-done = bf16[8,27,256]{2,0,1:T(8,128)(2,1)S(1)} copy-done((bf16[8,27,256]{2,0,1:T(8,128)(2,1)S(1)}, bf16[8,27,256]{2,0,1:T(8,128)(2,1)}, u32[]{:S(2)}) %copy-start) | copy-done | bytes 110616
  1.5 0.7 copy_bitcast_fusion.1.shard
  2.2 74.3 %shard_map.58 = (bf16[2,16,16,256]{3,2,1,0:T(8,128)(2,1)}, bf16[2,16,16,512]{3,2,1,0:T(8,128)(2,1)}, f32[2,27,8,128]{3,2,1,0:T(8,128)}) custom-call(bf16[2,16,16,512]{3,2,1,0:T(8,128)(2,1)} %bitcast.16, bf16[2,16,16,256]{3,2,1,0:T(8,128)(2,1)} %bitcast.17, bf16[2,27,8,128]{3,2,1,0:T(8,128)(2,1)} %copy_bitcast_fusion.1.shard), custom_call_target="tpu_custom_call" | custom-call | flops 11000000512 | bytes 4000000 | tf_op jit(solution)/shard_map/pallas_call | solution.py:455
  76.5 0.0 copy-start.1
  76.5 1.7 %copy_bitcast_fusion = f32[8,27,256]{2,0,1:T(8,128)} fusion(f32[2,27,8,128]{3,2,1,0:T(8,128)} %get-tuple-element.8), kind=kLoop, calls=%fused_computation | loop fusion | bytes 442368 | tf_op jit(solution)/shard_map/reshape | solution.py:495
  78.2 1.7 %copy.12 = bf16[1,2,16,16,256]{4,3,2,1,0:T(8,128)(2,1)} copy(bf16[1,2,16,16,256]{4,3,2,1,0:T(8,128)(2,1)} %bitcast.15) | data formatting | bytes 524288
  79.9 0.0 copy-done.1
  79.9 0.8 copy.13
Async XLA Ops:
  0.6 0.9 %copy-start = (bf16[8,27,256]{2,0,1:T(8,128)(2,1)S(1)}, bf16[8,27,256]{2,0,1:T(8,128)(2,1)}, u32[]{:S(2)}) copy-start(bf16[8,27,256]{2,0,1:T(8,128)(2,1)} %param.4) | copy-start | bytes 331780
  76.5 3.4 %copy-start.1 = (bf16[2,16,16,512]{3,2,1,0:T(8,128)(2,1)S(1)}, bf16[2,16,16,512]{3,2,1,0:T(8,128)(2,1)}, u32[]{:S(2)}) copy-start(bf16[2,16,16,512]{3,2,1,0:T(8,128)(2,1)} %get-tuple-element.7) | copy-start | bytes 1572868

commit v2 on v1

v2 whole, which is shorter than its diff:
```python
import jax
import jax.numpy as jnp
from jax import lax
from jax.experimental import pallas as pl
from jax.experimental.pallas import tpu as pltpu
from jax.sharding import PartitionSpec as P

MESH = pl.DeviceIdType.MESH
F32 = jnp.float32
BF16 = jnp.bfloat16
ORDERS = (("z", "x", "y"), ("y", "z", "x"), ("x", "y", "z"))
LOW, HIGH = pl.ds(0, 2), pl.ds(2, 2)
COPIES = 128


def silu(v):
    return v * jax.nn.sigmoid(v)


def step_kernel(
    acts,
    cot,
    shard,
    outputs,
    grad_input,
    grad_kernel,
    weights,
    partial,
    from_partner,
    rx3p,
    rx3m,
    rx2p,
    rx2m,
    rx1,
    own_sum,
    other_sum,
    final_own,
    final_other,
    hidden3,
    cot3,
    hidden_t,
    halo_cot,
    edge_out,
    edge_in,
    acc_out,
    acc_back,
    send_sem,
    recv_sem,
    local_sem,
):
    space, fsdp = lax.axis_index("space"), lax.axis_index("fsdp")
    core, z_hi = space % 2, space // 2
    y, x, zl = fsdp // 16, (fsdp // 4) % 4, fsdp % 4
    z = z_hi * 4 + zl
    own = {"y": y, "x": x, "z": zl}

    def neighbour(dim, delta):
        if dim == "y":
            return (space, ((y + 4 + delta) % 4) * 16 + x * 4 + zl)
        if dim == "x":
            return (space, y * 16 + ((x + 4 + delta) % 4) * 4 + zl)
        there = (z + 8 + delta) % 8
        return ((there // 4) * 2 + core, y * 16 + x * 4 + there % 4)

    partner = (z_hi * 2 + 1 - core, fsdp)
    across = ((space + 2) % 4, fsdp)
    greeted = [neighbour(d, k) for d in ("y", "x") for k in (1, -1, 2)]
    greeted += [neighbour("z", k) for k in (1, -1, 2, -2)]
    greeted += [partner, across, (3 - space, fsdp)]

    barrier = pltpu.get_barrier_semaphore()
    for device in greeted:
        pl.semaphore_signal(barrier, inc=1, device_id=device, device_id_type=MESH)

    counter = [0]
    sent = []

    def remote(src, dst, device):
        number = counter[0]
        counter[0] += 1
        return pltpu.make_async_remote_copy(
            src_ref=src,
            dst_ref=dst,
            send_sem=send_sem.at[number],
            recv_sem=recv_sem.at[number],
            device_id=device,
            device_id_type=MESH,
        )

    def send(src, dst, device):
        copy = remote(src, dst, device)
        copy.start()
        sent.append(copy)
        return copy

    def at(dim, delta):
        return (own[dim] + 4 + delta) % 4

    def place(colour, first, second, third):
        d1, d2, d3 = ORDERS[colour]
        index = {d1: first, d2: second, d3: third}
        return index["y"], index["x"], index["z"]

    every = slice(None)

    lanes = pl.ds(pl.multiple_of(core * 128, 128), 128)
    other_lanes = pl.ds(pl.multiple_of((1 - core) * 128, 128), 128)

    def down_copy(src, dst):
        return remote(src, dst, (space - 1, fsdp))

    def up_copy(src, dst):
        return remote(src, dst, (space + 1, fsdp))

    def when_low(action):
        pl.when(space > 0)(action)

    def when_high(action):
        pl.when(space < 3)(action)

    cot_down = down_copy(cot.at[0], halo_cot.at[1])
    cot_up = up_copy(cot.at[1], halo_cot.at[0])
    edge_down = down_copy(edge_out.at[0], edge_in.at[1])
    edge_up = up_copy(edge_out.at[1], edge_in.at[0])

    def slot(colour, first, second, third):
        iy, ix, iz = place(colour, first, second, third)
        return weights.at[core, pl.ds(9 * colour, 9), iy, ix, iz]

    waiting = {}

    def spread(key, colour, where, device):
        piece = slot(colour, *where)
        waiting.setdefault(key, []).append(send(piece, piece, device))

    def take(key):
        for copy in waiting.pop(key):
            copy.wait_recv()

    def gather_0(colour):
        d1, d2, d3 = ORDERS[colour]
        here = slot(colour, own[d1], own[d2], own[d3])
        for delta in (1, -1, 2):
            copy = send(shard.at[pl.ds(9 * colour, 9), :, lanes], here, neighbour(d1, delta))
            waiting.setdefault(f"a1{colour}", []).append(copy)

    def gather_1(colour):
        d1, d2, d3 = ORDERS[colour]
        take(f"a1{colour}")
        for delta in (1, -1):
            spread(f"a2{colour}", colour, (every, own[d2], own[d3]), neighbour(d2, delta))

    def gather_2(colour):
        d1, d2, d3 = ORDERS[colour]
        take(f"a2{colour}")
        spread(f"a3{colour}", colour, (LOW, at(d2, -1), own[d3]), neighbour(d2, 1))
        spread(f"a3{colour}", colour, (HIGH, at(d2, 1), own[d3]), neighbour(d2, -1))

    def gather_3(colour):
        d1, d2, d3 = ORDERS[colour]
        take(f"a3{colour}")
        for delta in (1, -1):
            spread(f"a4{colour}", colour, (every, every, own[d3]), neighbour(d3, delta))
        spread(f"pair{colour}", colour, (every, every, own[d3]), partner)

    def gather_4(colour):
        d1, d2, d3 = ORDERS[colour]
        take(f"a4{colour}")
        spread(f"a5{colour}", colour, (LOW, every, at(d3, -1)), neighbour(d3, 1))
        spread(f"a5{colour}", colour, (HIGH, every, at(d3, 1)), neighbour(d3, -1))
        for delta in (1, -1):
            spread(f"pair{colour}", colour, (every, every, at(d3, delta)), partner)

    def gather_5(colour):
        d1, d2, d3 = ORDERS[colour]
        take(f"a5{colour}")
        spread(f"pair{colour}", colour, (LOW, every, at(d3, 2)), partner)
        spread(f"pair{colour}", colour, (HIGH, every, at(d3, 2)), partner)

    def gather_6(colour):
        take(f"pair{colour}")

    def term(ref, colour, first, second, third, taps=None):
        iy, ix, iz = place(colour, first, second, third)
        taps = pl.ds(9 * colour, 9) if taps is None else taps
        if ref is partial:
            return (core, taps, iy, ix, iz)
        return (taps, iy, ix, iz)

    def pass_on(key, colour, where, dst, device):
        src = partial.at[term(partial, colour, *where)]
        copy = send(src, dst.at[term(dst, colour, *where)], device)
        waiting.setdefault(key, []).append(copy)

    def add(colour, where, *others):
        def one(tap, carry):
            tap = tap + 9 * colour
            mine = term(partial, colour, *where, taps=tap)
            total = partial[mine].astype(F32)
            for ref in others:
                total = total + ref[term(ref, colour, *where, taps=tap)].astype(F32)
            partial[mine] = total.astype(BF16)
            return carry

        lax.fori_loop(0, 9, one, 0)

    def reduce_pair(key, tap, count):
        taps = pl.ds(tap, count)
        copy = send(partial.at[1 - core, taps], from_partner.at[taps], partner)
        waiting.setdefault(key, []).append(copy)

    def reduce_phase(phase, part, colour):
        plus, minus = (rx3p, rx3m) if phase == 3 else (rx2p, rx2m)
        order = ORDERS[colour]
        dim = order[phase - 1]
        forward, backward = neighbour(dim, 1), neighbour(dim, -1)
        far, near = f"far{phase}{colour}", f"near{phase}{colour}"

        def where(half, delta):
            if phase == 3:
                return (half, every, at(dim, delta))
            return (half, at(dim, delta), own[order[2]])

        if part == 0:
            pass_on(far, colour, where(LOW, 2), plus, forward)
            pass_on(far, colour, where(HIGH, 2), minus, backward)
            pass_on(near, colour, where(HIGH, 1), plus, forward)
            pass_on(near, colour, where(LOW, -1), minus, backward)
        elif part == 1:
            take(far)
            add(colour, where(LOW, 1), plus)
            pass_on(near, colour, where(LOW, 1), plus, forward)
            add(colour, where(HIGH, -1), minus)
            pass_on(near, colour, where(HIGH, -1), minus, backward)
        else:
            take(near)
            add(colour, where(every, 0), plus, minus)

    def reduce_1(colour):
        for key in ("p1",) if colour == 1 else ("p first", "p second"):
            if key in waiting:
                take(key)
        add(colour, (every, every, every), from_partner)
        reduce_phase(3, 0, colour)

    def reduce_2(colour):
        reduce_phase(3, 1, colour)

    def reduce_3(colour):
        reduce_phase(3, 2, colour)
        reduce_phase(2, 0, colour)

    def reduce_4(colour):
        reduce_phase(2, 1, colour)

    def reduce_5(colour):
        reduce_phase(2, 2, colour)
        d1, d2, d3 = ORDERS[colour]
        for number, delta in enumerate((1, -1, 2)):
            src = partial.at[term(partial, colour, at(d1, delta), own[d2], own[d3])]
            dst = rx1.at[number, pl.ds(9 * colour, 9)]
            copy = send(src, dst, neighbour(d1, delta))
            waiting.setdefault(f"r6{colour}", []).append(copy)

    def reduce_6(colour):
        take(f"r6{colour}")
        for tap in range(9 * colour, 9 * colour + 9):
            total = partial[core, tap, y, x, zl].astype(F32)
            for number in range(3):
                total = total + rx1[number, tap].astype(F32)
            own_sum[tap] = total.astype(BF16)
        taps = pl.ds(9 * colour, 9)
        waiting[f"r7{colour}"] = [send(own_sum.at[taps], other_sum.at[taps], across)]

    def reduce_7(scale):
        for colour in range(3):
            take(f"r7{colour}")
        final_own[...] = (own_sum[...].astype(F32) + other_sum[...].astype(F32)) * scale
        waiting["r8"] = [send(final_own, final_other, partner)]
        grad_kernel[:, :, lanes] = final_own[...]

    def reduce_8():
        take("r8")
        grad_kernel[:, :, other_lanes] = final_other[...]

    def shifted(values):
        rows = values.shape[0]
        w = lax.broadcasted_iota(jnp.int32, values.shape, 0) % 16
        before = jnp.where(w == 0, 0.0, pltpu.roll(values, 1, axis=0))
        after = jnp.where(w == 15, 0.0, pltpu.roll(values, rows - 1, axis=0))
        return before.astype(BF16), values.astype(BF16), after.astype(BF16)

    def put_hidden(values, d, h, count):
        for number, part in enumerate(shifted(values)):
            hidden3[number, d, pl.ds(h, count)] = part.reshape(count, 16, 512)

    def put_cot(values, d, h, count):
        for number, part in enumerate(shifted(values)):
            cot3[2 - number, d, pl.ds(h, count)] = part.reshape(count, 16, 256)

    def prepare_cot():
        for ref, width in ((cot3, 256), (hidden3, 512)):
            edge = jnp.zeros((3, ref.shape[1], 16, width), BF16)
            ref[:, :, 0] = edge
            ref[:, :, 17] = edge

        def one(i, carry):
            d, h = i // 4, (i % 4) * 4
            values = cot[d, pl.ds(h, 4)].astype(F32).reshape(64, 256)
            put_cot(values, d + 1, h + 1, 4)
            return carry

        lax.fori_loop(0, 8, one, 0)

    def prepare_hidden():
        for i in range(4):
            d, h = i // 2, (i % 2) * 8
            values = silu(acts[d, pl.ds(h, 8)].astype(F32).reshape(128, 512))
            put_hidden(values, d, h + 1, 8)
            hidden_t[:, 128 * i : 128 * i + 128] = values.T.astype(BF16)

    def fill_halo(side):
        (cot_down if side else cot_up).wait_recv()

        def one(i, carry):
            values = halo_cot[side, pl.ds(i * 4, 4)].astype(F32).reshape(64, 256)
            put_cot(values, 3 * side, i * 4 + 1, 4)
            return carry

        lax.fori_loop(0, 4, one, 0)

    def fill_near():
        for side in range(2):
            pl.when(core == 1 - side)(lambda: fill_halo(side))

    def fill_far():
        pl.when(space == 1)(lambda: fill_halo(1))
        pl.when(space == 2)(lambda: fill_halo(0))

    def no_halo():
        for side in range(2):

            @pl.when(space == 3 * side)
            def _():
                cot3[:, 3 * side] = jnp.zeros((3, 18, 16, 256), BF16)
                edge_in[side] = jnp.zeros((256, 256), BF16)

    def cot_rows(colour, b, number):
        rows = cot3[number, pl.ds(2 - colour, 2), pl.ds(2 - b, 16)]
        return rows.reshape(512, 256)

    def kernel_term(colour, b):
        rows = [cot_rows(colour, b, number) for number in range(3)]
        product = jnp.dot(
            hidden_t[...], jnp.concatenate(rows, axis=1), preferred_element_type=F32
        )
        for number in range(3):
            for half in range(2):
                start = 256 * number + 128 * half
                part = product[:, start : start + 128].reshape(4, 4, 4, 8, 128)
                partial[half, 9 * colour + 3 * b + number] = part.astype(BF16)

    def tap_weight(tap):
        halves = [weights[half, tap].reshape(512, 128) for half in range(2)]
        return jnp.concatenate(halves, axis=1)

    def forward_and_back(colour, b):
        taps = [tap_weight(9 * colour + 3 * b + number) for number in range(3)]
        rows = [hidden3[number, :, pl.ds(b, 16)].reshape(512, 512) for number in range(3)]
        product = jnp.dot(
            jnp.concatenate(rows, axis=1),
            jnp.concatenate(taps, axis=0),
            preferred_element_type=F32,
        )
        acc_out[colour] = product if b == 0 else acc_out[colour] + product
        grads = [cot_rows(colour, b, number) for number in range(3)]
        product = lax.dot_general(
            jnp.concatenate(grads, axis=1),
            jnp.concatenate(taps, axis=1),
            (((1,), (1,)), ((), ())),
            preferred_element_type=F32,
        )
        acc_back[...] = product if colour == 0 and b == 0 else acc_back[...] + product

    def send_edge_up():
        edge_out[1] = acc_out[0, 256:].astype(BF16)
        when_high(edge_up.start)

    def send_edge_down():
        edge_out[0] = acc_out[2, :256].astype(BF16)
        when_low(edge_down.start)

    def write_outputs():
        when_low(edge_up.wait_recv)
        total = acc_out[1, :256] + acc_out[2, 256:] + edge_in[0].astype(F32)
        outputs[0] = total.astype(BF16).reshape(16, 16, 256)
        when_high(edge_down.wait_recv)
        total = acc_out[1, 256:] + acc_out[0, :256] + edge_in[1].astype(F32)
        outputs[1] = total.astype(BF16).reshape(16, 16, 256)

    def write_grad_input():
        for i in range(8):
            d, h = i // 4, (i % 4) * 4
            values = acts[d, pl.ds(h, 4)].astype(F32).reshape(64, 512)
            squash = jax.nn.sigmoid(values)
            slope = squash * (1.0 + values * (1.0 - squash))
            total = acc_back[64 * i : 64 * i + 64] * slope
            grad_input[d, pl.ds(h, 4)] = total.astype(BF16).reshape(4, 16, 512)

    def finish():
        for copy in sent:
            copy.wait_send()

        @when_low
        def _():
            cot_down.wait_send()
            edge_down.wait_send()

        @when_high
        def _():
            cot_up.wait_send()
            edge_up.wait_send()

    first, second = 2 - 2 * z_hi, 2 * z_hi

    def near_term(b):
        kernel_term(first, b)
        reduce_pair("p first", 9 * first + 3 * b, 3)

    def far_term(b):
        kernel_term(second, b)
        reduce_pair("p second", 9 * second + 3 * b, 3)

    prepare_cot()
    prepare_hidden()
    no_halo()
    kernel_term(1, 0)
    kernel_term(1, 1)
    kernel_term(1, 2)
    pl.semaphore_wait(barrier, len(greeted))
    gather_0(0)
    gather_0(1)
    gather_0(2)
    when_low(cot_down.start)
    when_high(cot_up.start)
    mine = pltpu.make_async_copy(
        shard.at[:, :, lanes], weights.at[core, :, y, x, zl], local_sem
    )
    mine.start()
    reduce_pair("p1", 9, 9)
    fill_near()
    near_term(0)
    near_term(1)
    near_term(2)
    mine.wait()
    gather_1(1)
    gather_1(2)
    gather_1(0)
    fill_far()
    far_term(0)
    far_term(1)
    gather_2(2)
    gather_2(1)
    gather_2(0)
    far_term(2)
    reduce_1(1)
    reduce_1(0)
    reduce_1(2)
    gather_3(2)
    gather_3(1)
    gather_3(0)
    reduce_2(1)
    reduce_2(0)
    reduce_2(2)
    gather_4(1)
    gather_4(0)
    gather_4(2)
    reduce_3(1)
    reduce_3(0)
    reduce_3(2)
    reduce_4(1)
    gather_5(1)
    gather_5(0)
    gather_5(2)
    reduce_4(0)
    reduce_4(2)
    gather_6(0)
    forward_and_back(0, 0)
    reduce_5(1)
    forward_and_back(0, 1)
    reduce_5(0)
    forward_and_back(0, 2)
    send_edge_up()
    reduce_5(2)
    gather_6(2)
    forward_and_back(2, 0)
    reduce_6(1)
    forward_and_back(2, 1)
    reduce_6(0)
    forward_and_back(2, 2)
    send_edge_down()
    reduce_6(2)
    gather_6(1)
    forward_and_back(1, 0)
    forward_and_back(1, 1)
    forward_and_back(1, 2)
    write_grad_input()
    reduce_7(1.0 / lax.axis_size("fsdp"))
    write_outputs()
    reduce_8()
    finish()


def write_kernel(outputs, grad_input, grad_kernel, outputs_to, grad_input_to, grad_kernel_to):
    outputs_to[...] = outputs[...]
    grad_input_to[...] = grad_input[...]
    grad_kernel_to[...] = grad_kernel[...]


def body(acts, kernel, cotangent):
    vmem = pl.BlockSpec(memory_space=pltpu.VMEM)
    whole = (27, 4, 4, 4, 8, 128)
    results = (
        jax.ShapeDtypeStruct((2, 16, 16, 256), BF16),
        jax.ShapeDtypeStruct((2, 16, 16, 512), BF16),
        jax.ShapeDtypeStruct((27, 8, 256), F32),
    )
    computed = pl.pallas_call(
        step_kernel,
        out_shape=results,
        in_specs=[vmem] * 3,
        out_specs=(vmem,) * 3,
        scratch_shapes=[
            pltpu.VMEM((2, *whole), BF16),
            pltpu.VMEM((2, *whole), BF16),
            pltpu.VMEM(whole, BF16),
            pltpu.VMEM(whole, BF16),
            pltpu.VMEM(whole, BF16),
            pltpu.VMEM(whole, BF16),
            pltpu.VMEM(whole, BF16),
            pltpu.VMEM((3, 27, 8, 128), BF16),
            pltpu.VMEM((27, 8, 128), BF16),
            pltpu.VMEM((27, 8, 128), BF16),
            pltpu.VMEM((27, 8, 128), F32),
            pltpu.VMEM((27, 8, 128), F32),
            pltpu.VMEM((3, 2, 18, 16, 512), BF16),
            pltpu.VMEM((3, 4, 18, 16, 256), BF16),
            pltpu.VMEM((512, 512), BF16),
            pltpu.VMEM((2, 16, 16, 256), BF16),
            pltpu.VMEM((2, 256, 256), BF16),
            pltpu.VMEM((2, 256, 256), BF16),
            pltpu.VMEM((3, 512, 256), F32),
            pltpu.VMEM((512, 512), F32),
            pltpu.SemaphoreType.DMA((COPIES,)),
            pltpu.SemaphoreType.DMA((COPIES,)),
            pltpu.SemaphoreType.DMA,
        ],
        compiler_params=pltpu.CompilerParams(
            collective_id=0, has_side_effects=True, vmem_limit_bytes=54_000_000
        ),
        cost_estimate=pl.CostEstimate(
            flops=11_000_000_000, bytes_accessed=4_000_000, transcendentals=1_000_000
        ),
    )(acts[0], cotangent[0], kernel.transpose(1, 0, 2))
    outputs, grad_input, grad_kernel = pl.pallas_call(
        write_kernel,
        out_shape=results,
        in_specs=[vmem] * 3,
        out_specs=(vmem,) * 3,
        compiler_params=pltpu.CompilerParams(vmem_limit_bytes=8_000_000),
    )(*computed)
    return outputs[None], grad_input[None], grad_kernel.transpose(1, 0, 2)


def solution(mesh):
    return jax.shard_map(
        body,
        mesh=mesh,
        in_specs=(
            P("fsdp", "space", None, None, None),
            P("fsdp", None, None),
            P("fsdp", "space", None, None, None),
        ),
        out_specs=(
            P("fsdp", "space", None, None, None),
            P("fsdp", "space", None, None, None),
            P("fsdp", None, None),
        ),
        check_vma=False,
    )
```

time: 82.3 us -> 71.8 us (0.87)
  the two profiles are of different devices: /device:TPU:3 before, /device:TPU:33 now
where the time goes in v2:
time: 71.8 us; the launch traced here: 71.6 us
  Pallas kernels  68 us (95%)
  local copies, waits for them, and re-layouts  2.88 us (4%)
    pallas_call x1, Pallas kernels, body(): pl.pallas_call(step_kernel, out_shape=results, in_specs=[vmem] * 3, out_s...  67 us
    unnamed x6, local copies, waits for them, and re-layouts  2.88 us

profile of v2, /device:TPU:33, one launch (start us, length us, event | category | flops | bytes accessed | tf_op | source)
XLA Modules:
  0.0 71.6 jit_solution(17302411083415495520)
XLA Ops:
  0.6 0.0 copy-start
  0.6 1.0 %copy-done = bf16[1,2,16,16,512]{4,3,2,1,0:T(8,128)(2,1)S(1)} copy-done((bf16[1,2,16,16,512]{4,3,2,1,0:T(8,128)(2,1)S(1)}, bf16[1,2,16,16,512]{4,3,2,1,0:T(8,128)(2,1)}, u32[]{:S(2)}) %copy-start) | copy-done | bytes 524312
  1.7 0.0 copy-start.1
  1.7 0.9 %copy-done.1 = bf16[1,2,16,16,256]{4,3,2,1,0:T(8,128)(2,1)S(1)} copy-done((bf16[1,2,16,16,256]{4,3,2,1,0:T(8,128)(2,1)S(1)}, bf16[1,2,16,16,256]{4,3,2,1,0:T(8,128)(2,1)}, u32[]{:S(2)}) %copy-start.1) | copy-done | bytes 262168
  2.6 0.0 copy-start.2
  2.6 0.9 %copy-done.2 = bf16[8,27,256]{2,0,1:T(8,128)(2,1)S(1)} copy-done((bf16[8,27,256]{2,0,1:T(8,128)(2,1)S(1)}, bf16[8,27,256]{2,0,1:T(8,128)(2,1)}, u32[]{:S(2)}) %copy-start.2) | copy-done | bytes 110616
  3.5 67.0 %shard_map.58 = (bf16[2,16,16,256]{3,2,1,0:T(8,128)(2,1)S(1)}, bf16[2,16,16,512]{3,2,1,0:T(8,128)(2,1)S(1)}, f32[27,8,256]{2,1,0:T(8,128)S(1)}) custom-call(bf16[2,16,16,512]{3,2,1,0:T(8,128)(2,1)S(1)} %bitcast.6, bf16[2,16,16,256]{3,2,1,0:T(8,128)(2,1)S(1)} %bitcast.7, bf16[27,8,256]{2,1,0:T(8,128)(2,1)S(1)} %bitcast.8), custom_call_target="tpu_custom_call" | custom-call | flops 11000000512 | bytes 4000000 | tf_op jit(solution)/shard_map/pallas_call | solution.py:528
  70.6 1.0 %shard_map.59 = (bf16[2,16,16,256]{3,2,1,0:T(8,128)(2,1)}, bf16[2,16,16,512]{3,2,1,0:T(8,128)(2,1)}, f32[27,8,256]{2,1,0:T(8,128)}) custom-call(bf16[2,16,16,256]{3,2,1,0:T(8,128)(2,1)S(1)} %get-tuple-element.9.outputs, bf16[2,16,16,512]{3,2,1,0:T(8,128)(2,1)S(1)} %get-tuple-element.10.grad_input, f32[27,8,256]{2,1,0:T(8,128)S(1)} %get-tuple-element.11.grad_kernel), custom_call_target="tpu_custom_call" | custom-call | tf_op jit(solution)/shard_map/pallas_call | solution.py:565
Async XLA Ops:
  0.6 1.0 %copy-start = (bf16[1,2,16,16,512]{4,3,2,1,0:T(8,128)(2,1)S(1)}, bf16[1,2,16,16,512]{4,3,2,1,0:T(8,128)(2,1)}, u32[]{:S(2)}) copy-start(bf16[1,2,16,16,512]{4,3,2,1,0:T(8,128)(2,1)} %param.3) | copy-start | bytes 1572868
  1.7 0.9 %copy-start.1 = (bf16[1,2,16,16,256]{4,3,2,1,0:T(8,128)(2,1)S(1)}, bf16[1,2,16,16,256]{4,3,2,1,0:T(8,128)(2,1)}, u32[]{:S(2)}) copy-start(bf16[1,2,16,16,256]{4,3,2,1,0:T(8,128)(2,1)} %param.5) | copy-start | bytes 786436
  2.6 0.9 %copy-start.2 = (bf16[8,27,256]{2,0,1:T(8,128)(2,1)S(1)}, bf16[8,27,256]{2,0,1:T(8,128)(2,1)}, u32[]{:S(2)}) copy-start(bf16[8,27,256]{2,0,1:T(8,128)(2,1)} %param.4) | copy-start | bytes 331780

commit v3 on v2

--- a/solution.py
+++ b/solution.py
@@ -18,9 +18,9 @@
 
 
 def step_kernel(
-    acts,
-    cot,
-    shard,
+    acts_in,
+    cot_in,
+    shard_in,
     outputs,
     grad_input,
     grad_kernel,
@@ -42,8 +42,12 @@
     halo_cot,
     edge_out,
     edge_in,
-    acc_out,
+    acc_edge,
+    acc_mid,
     acc_back,
+    acts,
+    cot,
+    shard,
     send_sem,
     recv_sem,
     local_sem,
@@ -67,6 +71,13 @@
     greeted = [neighbour(d, k) for d in ("y", "x") for k in (1, -1, 2)]
     greeted += [neighbour("z", k) for k in (1, -1, 2, -2)]
     greeted += [partner, across, (3 - space, fsdp)]
+
+    shard_copy = pltpu.make_async_copy(shard_in, shard, local_sem.at[1])
+    cot_copy = pltpu.make_async_copy(cot_in, cot, local_sem.at[2])
+    acts_copy = pltpu.make_async_copy(acts_in, acts, local_sem.at[3])
+    shard_copy.start()
+    cot_copy.start()
+    acts_copy.start()
 
     barrier = pltpu.get_barrier_semaphore()
     for device in greeted:
@@ -159,23 +170,29 @@
     def gather_3(colour):
         d1, d2, d3 = ORDERS[colour]
         take(f"a3{colour}")
-        for delta in (1, -1):
-            spread(f"a4{colour}", colour, (every, every, own[d3]), neighbour(d3, delta))
+        spread(f"a4{colour}", colour, (LOW, every, own[d3]), neighbour(d3, 1))
+        spread(f"a4{colour}", colour, (HIGH, every, own[d3]), neighbour(d3, -1))
         spread(f"pair{colour}", colour, (every, every, own[d3]), partner)
+
+    def gather_3b(colour):
+        d1, d2, d3 = ORDERS[colour]
+        spread(f"a5{colour}", colour, (HIGH, every, own[d3]), neighbour(d3, 1))
+        spread(f"a5{colour}", colour, (LOW, every, own[d3]), neighbour(d3, -1))
 
     def gather_4(colour):
         d1, d2, d3 = ORDERS[colour]
         take(f"a4{colour}")
         spread(f"a5{colour}", colour, (LOW, every, at(d3, -1)), neighbour(d3, 1))
         spread(f"a5{colour}", colour, (HIGH, every, at(d3, 1)), neighbour(d3, -1))
-        for delta in (1, -1):
-            spread(f"pair{colour}", colour, (every, every, at(d3, delta)), partner)
+        spread(f"pair{colour}", colour, (LOW, every, at(d3, -1)), partner)
+        spread(f"pair{colour}", colour, (HIGH, every, at(d3, 1)), partner)
 
     def gather_5(colour):
         d1, d2, d3 = ORDERS[colour]
         take(f"a5{colour}")
-        spread(f"pair{colour}", colour, (LOW, every, at(d3, 2)), partner)
-        spread(f"pair{colour}", colour, (HIGH, every, at(d3, 2)), partner)
+        spread(f"pair{colour}", colour, (HIGH, every, at(d3, -1)), partner)
+        spread(f"pair{colour}", colour, (LOW, every, at(d3, 1)), partner)
+        spread(f"pair{colour}", colour, (every, every, at(d3, 2)), partner)
 
     def gather_6(colour):
         take(f"pair{colour}")
@@ -221,9 +238,10 @@
                 return (half, every, at(dim, delta))
             return (half, at(dim, delta), own[order[2]])
 
-        if part == 0:
+        if part == "far":
             pass_on(far, colour, where(LOW, 2), plus, forward)
             pass_on(far, colour, where(HIGH, 2), minus, backward)
+        elif part == "near":
             pass_on(near, colour, where(HIGH, 1), plus, forward)
             pass_on(near, colour, where(LOW, -1), minus, backward)
         elif part == 1:
@@ -241,14 +259,18 @@
             if key in waiting:
                 take(key)
         add(colour, (every, every, every), from_partner)
-        reduce_phase(3, 0, colour)
+        reduce_phase(3, "far", colour)
+
+    def reduce_1b(colour):
+        reduce_phase(3, "near", colour)
 
     def reduce_2(colour):
         reduce_phase(3, 1, colour)
 
     def reduce_3(colour):
         reduce_phase(3, 2, colour)
-        reduce_phase(2, 0, colour)
+        reduce_phase(2, "far", colour)
+        reduce_phase(2, "near", colour)
 
     def reduce_4(colour):
         reduce_phase(2, 1, colour)
@@ -364,38 +386,54 @@
         halves = [weights[half, tap].reshape(512, 128) for half in range(2)]
         return jnp.concatenate(halves, axis=1)
 
-    def forward_and_back(colour, b):
-        taps = [tap_weight(9 * colour + 3 * b + number) for number in range(3)]
+    def three_taps(colour, b):
+        return [tap_weight(9 * colour + 3 * b + number) for number in range(3)]
+
+    def hidden_rows(b):
         rows = [hidden3[number, :, pl.ds(b, 16)].reshape(512, 512) for number in range(3)]
-        product = jnp.dot(
-            jnp.concatenate(rows, axis=1),
-            jnp.concatenate(taps, axis=0),
-            preferred_element_type=F32,
-        )
-        acc_out[colour] = product if b == 0 else acc_out[colour] + product
-        grads = [cot_rows(colour, b, number) for number in range(3)]
-        product = lax.dot_general(
+        return jnp.concatenate(rows, axis=1)
+
+    def back_product(colours, b, taps):
+        grads = [cot_rows(colour, b, number) for colour in colours for number in range(3)]
+        return lax.dot_general(
             jnp.concatenate(grads, axis=1),
             jnp.concatenate(taps, axis=1),
             (((1,), (1,)), ((), ())),
             preferred_element_type=F32,
         )
-        acc_back[...] = product if colour == 0 and b == 0 else acc_back[...] + product
-
-    def send_edge_up():
-        edge_out[1] = acc_out[0, 256:].astype(BF16)
+
+    def forward_edges(b):
+        below, above = three_taps(0, b), three_taps(2, b)
+        both = [jnp.concatenate(pair, axis=1) for pair in zip(below, above)]
+        product = jnp.dot(
+            hidden_rows(b), jnp.concatenate(both, axis=0), preferred_element_type=F32
+        )
+        acc_edge[...] = product if b == 0 else acc_edge[...] + product
+
+    def back_edges(b):
+        product = back_product((0, 2), b, three_taps(0, b) + three_taps(2, b))
+        acc_back[...] = product if b == 0 else acc_back[...] + product
+
+    def forward_and_back(b):
+        taps = three_taps(1, b)
+        product = jnp.dot(
+            hidden_rows(b), jnp.concatenate(taps, axis=0), preferred_element_type=F32
+        )
+        acc_mid[...] = product if b == 0 else acc_mid[...] + product
+        acc_back[...] = acc_back[...] + back_product((1,), b, taps)
+
+    def send_edges():
+        edge_out[1] = acc_edge[256:, :256].astype(BF16)
         when_high(edge_up.start)
-
-    def send_edge_down():
-        edge_out[0] = acc_out[2, :256].astype(BF16)
+        edge_out[0] = acc_edge[:256, 256:].astype(BF16)
         when_low(edge_down.start)
 
     def write_outputs():
         when_low(edge_up.wait_recv)
-        total = acc_out[1, :256] + acc_out[2, 256:] + edge_in[0].astype(F32)
+        total = acc_mid[:256] + acc_edge[256:, 256:] + edge_in[0].astype(F32)
         outputs[0] = total.astype(BF16).reshape(16, 16, 256)
         when_high(edge_down.wait_recv)
-        total = acc_out[1, 256:] + acc_out[0, :256] + edge_in[1].astype(F32)
+        total = acc_mid[256:] + acc_edge[:256, :256] + edge_in[1].astype(F32)
         outputs[1] = total.astype(BF16).reshape(16, 16, 256)
 
     def write_grad_input():
@@ -431,79 +469,87 @@
         kernel_term(second, b)
         reduce_pair("p second", 9 * second + 3 * b, 3)
 
+    pl.semaphore_wait(barrier, len(greeted))
+    shard_copy.wait()
+    gather_0(0)
+    gather_0(1)
+    gather_0(2)
+    cot_copy.wait()
+    when_low(cot_down.start)
+    when_high(cot_up.start)
+    mine = pltpu.make_async_copy(
+        shard.at[:, :, lanes], weights.at[core, :, y, x, zl], local_sem.at[0]
+    )
+    mine.start()
     prepare_cot()
+    acts_copy.wait()
     prepare_hidden()
     no_halo()
     kernel_term(1, 0)
     kernel_term(1, 1)
     kernel_term(1, 2)
-    pl.semaphore_wait(barrier, len(greeted))
-    gather_0(0)
-    gather_0(1)
-    gather_0(2)
-    when_low(cot_down.start)
-    when_high(cot_up.start)
-    mine = pltpu.make_async_copy(
-        shard.at[:, :, lanes], weights.at[core, :, y, x, zl], local_sem
-    )
-    mine.start()
     reduce_pair("p1", 9, 9)
     fill_near()
     near_term(0)
     near_term(1)
-    near_term(2)
     mine.wait()
     gather_1(1)
     gather_1(2)
     gather_1(0)
+    near_term(2)
     fill_far()
     far_term(0)
     far_term(1)
-    gather_2(2)
-    gather_2(1)
-    gather_2(0)
     far_term(2)
     reduce_1(1)
     reduce_1(0)
     reduce_1(2)
+    gather_2(2)
+    gather_2(1)
+    gather_2(0)
+    reduce_1b(1)
+    reduce_1b(0)
+    reduce_1b(2)
+    reduce_2(1)
+    reduce_2(0)
+    reduce_2(2)
     gather_3(2)
     gather_3(1)
     gather_3(0)
-    reduce_2(1)
-    reduce_2(0)
-    reduce_2(2)
-    gather_4(1)
-    gather_4(0)
-    gather_4(2)
     reduce_3(1)
     reduce_3(0)
     reduce_3(2)
+    gather_3b(2)
+    gather_3b(1)
+    gather_3b(0)
+    gather_4(2)
+    gather_4(1)
+    gather_4(0)
     reduce_4(1)
-    gather_5(1)
-    gather_5(0)
-    gather_5(2)
     reduce_4(0)
     reduce_4(2)
+    reduce_5(1)
+    reduce_5(0)
+    reduce_5(2)
+    gather_5(2)
+    gather_5(0)
+    gather_5(1)
+    gather_6(2)
     gather_6(0)
-    forward_and_back(0, 0)
-    reduce_5(1)
-    forward_and_back(0, 1)
-    reduce_5(0)
-    forward_and_back(0, 2)
-    send_edge_up()
-    reduce_5(2)
-    gather_6(2)
-    forward_and_back(2, 0)
+    forward_edges(0)
+    forward_edges(1)
+    forward_edges(2)
+    send_edges()
     reduce_6(1)
-    forward_and_back(2, 1)
     reduce_6(0)
-    forward_and_back(2, 2)
-    send_edge_down()
     reduce_6(2)
+    back_edges(0)
+    back_edges(1)
+    back_edges(2)
     gather_6(1)
-    forward_and_back(1, 0)
-    forward_and_back(1, 1)
-    forward_and_back(1, 2)
+    forward_and_back(0)
+    forward_and_back(1)
+    forward_and_back(2)
     write_grad_input()
     reduce_7(1.0 / lax.axis_size("fsdp"))
     write_outputs()
@@ -515,6 +561,10 @@
     outputs_to[...] = outputs[...]
     grad_input_to[...] = grad_input[...]
     grad_kernel_to[...] = grad_kernel[...]
+
+
+def in_hbm(value):
+    return pltpu.with_memory_space_constraint(value, pltpu.HBM)
 
 
 def body(acts, kernel, cotangent):
@@ -528,7 +578,7 @@
     computed = pl.pallas_call(
         step_kernel,
         out_shape=results,
-        in_specs=[vmem] * 3,
+        in_specs=[pl.BlockSpec(memory_space=pltpu.HBM)] * 3,
         out_specs=(vmem,) * 3,
         scratch_shapes=[
             pltpu.VMEM((2, *whole), BF16),
@@ -549,11 +599,15 @@
             pltpu.VMEM((2, 16, 16, 256), BF16),
             pltpu.VMEM((2, 256, 256), BF16),
             pltpu.VMEM((2, 256, 256), BF16),
-            pltpu.VMEM((3, 512, 256), F32),
             pltpu.VMEM((512, 512), F32),
+            pltpu.VMEM((512, 256), F32),
+            pltpu.VMEM((512, 512), F32),
+            pltpu.VMEM((2, 16, 16, 512), BF16),
+            pltpu.VMEM((2, 16, 16, 256), BF16),
+            pltpu.VMEM((27, 8, 256), BF16),
             pltpu.SemaphoreType.DMA((COPIES,)),
             pltpu.SemaphoreType.DMA((COPIES,)),
-            pltpu.SemaphoreType.DMA,
+            pltpu.SemaphoreType.DMA((4,)),
         ],
         compiler_params=pltpu.CompilerParams(
             collective_id=0, has_side_effects=True, vmem_limit_bytes=54_000_000
@@ -561,7 +615,7 @@
         cost_estimate=pl.CostEstimate(
             flops=11_000_000_000, bytes_accessed=4_000_000, transcendentals=1_000_000
         ),
-    )(acts[0], cotangent[0], kernel.transpose(1, 0, 2))
+    )(*(in_hbm(v) for v in (acts[0], cotangent[0], kernel.transpose(1, 0, 2))))
     outputs, grad_input, grad_kernel = pl.pallas_call(
         write_kernel,
         out_shape=results,

time: 71.8 us -> 64.5 us (0.90)
  the two profiles are of different devices: /device:TPU:33 before, /device:TPU:3 now
where the time goes in v3:
time: 64.5 us; the launch traced here: 64.4 us
  Pallas kernels  63.8 us (99%)
    pallas_call x1, Pallas kernels, body(): pl.pallas_call(step_kernel, out_shape=results, in_specs=[pl.BlockSpec(mem...  62.8 us

profile of v3, /device:TPU:3, one launch (start us, length us, event | category | flops | bytes accessed | tf_op | source)
XLA Modules:
  0.0 64.4 jit_solution(1292841486814518624)
XLA Ops:
  0.6 62.8 %shard_map.58 = (bf16[2,16,16,256]{3,2,1,0:T(8,128)(2,1)S(1)}, bf16[2,16,16,512]{3,2,1,0:T(8,128)(2,1)S(1)}, f32[27,8,256]{2,1,0:T(8,128)S(1)}) custom-call(bf16[2,16,16,512]{3,2,1,0:T(8,128)(2,1)} %bitcast.6, bf16[2,16,16,256]{3,2,1,0:T(8,128)(2,1)} %bitcast.8, bf16[27,8,256]{2,1,0:T(8,128)(2,1)} %bitcast.11), custom_call_target="tpu_custom_call" | custom-call | flops 11000000512 | bytes 4000000 | tf_op jit(solution)/shard_map/pallas_call | solution.py:578
  63.4 1.0 %shard_map.59 = (bf16[2,16,16,256]{3,2,1,0:T(8,128)(2,1)}, bf16[2,16,16,512]{3,2,1,0:T(8,128)(2,1)}, f32[27,8,256]{2,1,0:T(8,128)}) custom-call(bf16[2,16,16,256]{3,2,1,0:T(8,128)(2,1)S(1)} %get-tuple-element.9.outputs, bf16[2,16,16,512]{3,2,1,0:T(8,128)(2,1)S(1)} %get-tuple-element.10.grad_input, f32[27,8,256]{2,1,0:T(8,128)S(1)} %get-tuple-element.11.grad_kernel), custom_call_target="tpu_custom_call" | custom-call | tf_op jit(solution)/shard_map/pallas_call | solution.py:619

commit v4 on v3

--- a/solution.py
+++ b/solution.py
@@ -85,6 +85,7 @@
 
     counter = [0]
     sent = []
+    held = None
 
     def remote(src, dst, device):
         number = counter[0]
@@ -100,7 +101,10 @@
 
     def send(src, dst, device):
         copy = remote(src, dst, device)
-        copy.start()
+        if held is None:
+            copy.start()
+        else:
+            held.append(copy)
         sent.append(copy)
         return copy
 
@@ -157,7 +161,6 @@
 
     def gather_1(colour):
         d1, d2, d3 = ORDERS[colour]
-        take(f"a1{colour}")
         for delta in (1, -1):
             spread(f"a2{colour}", colour, (every, own[d2], own[d3]), neighbour(d2, delta))
 
@@ -255,7 +258,7 @@
             add(colour, where(every, 0), plus, minus)
 
     def reduce_1(colour):
-        for key in ("p1",) if colour == 1 else ("p first", "p second"):
+        for key in ("p1",) if colour == 1 else ("p second",):
             if key in waiting:
                 take(key)
         add(colour, (every, every, every), from_partner)
@@ -393,34 +396,50 @@
         rows = [hidden3[number, :, pl.ds(b, 16)].reshape(512, 512) for number in range(3)]
         return jnp.concatenate(rows, axis=1)
 
-    def back_product(colours, b, taps):
+    def add_back(colours, b, taps, first=False):
         grads = [cot_rows(colour, b, number) for colour in colours for number in range(3)]
-        return lax.dot_general(
-            jnp.concatenate(grads, axis=1),
-            jnp.concatenate(taps, axis=1),
-            (((1,), (1,)), ((), ())),
-            preferred_element_type=F32,
-        )
+        grads, taps = jnp.concatenate(grads, axis=1), jnp.concatenate(taps, axis=1)
+        for start in (0, 256):
+            product = lax.dot_general(
+                grads,
+                taps[start : start + 256],
+                (((1,), (1,)), ((), ())),
+                preferred_element_type=F32,
+            )
+            there = (slice(None), slice(start, start + 256))
+            acc_back[there] = product if first else acc_back[there] + product
+
+    def rows_of(d, b):
+        rows = [hidden3[number, d, pl.ds(b, 16)].reshape(256, 512) for number in range(3)]
+        return jnp.concatenate(rows, axis=1)
+
+    def forward_part(b, below_d, above_d):
+        for colour, d in ((0, below_d), (2, above_d)):
+            product = jnp.dot(
+                rows_of(d, b),
+                jnp.concatenate(three_taps(colour, b), axis=0),
+                preferred_element_type=F32,
+            )
+            there = (pl.ds(256 * d, 256), pl.ds(128 * colour, 256))
+            acc_edge[there] = product if b == 0 else acc_edge[there] + product
 
     def forward_edges(b):
-        below, above = three_taps(0, b), three_taps(2, b)
-        both = [jnp.concatenate(pair, axis=1) for pair in zip(below, above)]
-        product = jnp.dot(
-            hidden_rows(b), jnp.concatenate(both, axis=0), preferred_element_type=F32
-        )
-        acc_edge[...] = product if b == 0 else acc_edge[...] + product
+        forward_part(b, 1, 0)
+
+    def forward_inner(b):
+        forward_part(b, 0, 1)
 
     def back_edges(b):
-        product = back_product((0, 2), b, three_taps(0, b) + three_taps(2, b))
-        acc_back[...] = product if b == 0 else acc_back[...] + product
+        add_back((0, 2), b, three_taps(0, b) + three_taps(2, b), b == 0)
 
     def forward_and_back(b):
         taps = three_taps(1, b)
-        product = jnp.dot(
-            hidden_rows(b), jnp.concatenate(taps, axis=0), preferred_element_type=F32
-        )
-        acc_mid[...] = product if b == 0 else acc_mid[...] + product
-        acc_back[...] = acc_back[...] + back_product((1,), b, taps)
+        weight = jnp.concatenate(taps, axis=0)
+        for d in range(2):
+            product = jnp.dot(rows_of(d, b), weight, preferred_element_type=F32)
+            there = pl.ds(256 * d, 256)
+            acc_mid[there] = product if b == 0 else acc_mid[there] + product
+        add_back((1,), b, taps)
 
     def send_edges():
         edge_out[1] = acc_edge[256:, :256].astype(BF16)
@@ -446,8 +465,7 @@
             grad_input[d, pl.ds(h, 4)] = total.astype(BF16).reshape(4, 16, 512)
 
     def finish():
-        for copy in sent:
-            copy.wait_send()
+        drain()
 
         @when_low
         def _():
@@ -459,15 +477,66 @@
             cot_up.wait_send()
             edge_up.wait_send()
 
-    first, second = 2 - 2 * z_hi, 2 * z_hi
-
-    def near_term(b):
-        kernel_term(first, b)
-        reduce_pair("p first", 9 * first + 3 * b, 3)
-
-    def far_term(b):
-        kernel_term(second, b)
-        reduce_pair("p second", 9 * second + 3 * b, 3)
+    def all_terms():
+        nonlocal held
+        held = []
+        reduce_pair("p1", 9, 9)
+        for colour in (1, 2, 0):
+            gather_1(colour)
+        middle, *second_sends = held
+        held = None
+        pieces = []
+        base = counter[0]
+        counter[0] += 6
+
+        def piece(number, tap, count):
+            taps = pl.ds(tap, count)
+            return pltpu.make_async_remote_copy(
+                src_ref=partial.at[1 - core, taps],
+                dst_ref=from_partner.at[taps],
+                send_sem=send_sem.at[base + number],
+                recv_sem=recv_sem.at[base + number],
+                device_id=partner,
+                device_id_type=MESH,
+            )
+
+        def one(i, carry):
+            group, b = i // 3, i % 3
+            colour = 1 + ((group + 1) // 2) * (1 - 2 * z_hi) * (3 - 2 * group)
+
+            @pl.when(i == 3)
+            def _():
+                middle.start()
+                fill_near()
+
+            @pl.when(i == 5)
+            def _():
+                mine.wait()
+                for number, colour in enumerate((1, 2, 0)):
+                    take(f"a1{colour}")
+                    for copy in second_sends[2 * number : 2 * number + 2]:
+                        copy.start()
+
+            pl.when(i == 6)(fill_far)
+            kernel_term(colour, b)
+
+            @pl.when(i >= 3)
+            def _():
+                piece(i - 3, 9 * colour + 3 * b, 3).start()
+
+            return carry
+
+        lax.fori_loop(0, 9, one, 0)
+        for number in range(6):
+            tap = 9 * (2 - 2 * z_hi if number < 3 else 2 * z_hi) + 3 * (number % 3)
+            pieces.append(piece(number, tap, 3))
+        waiting["p second"] = pieces
+        sent.extend(pieces)
+
+    def drain():
+        for copy in sent:
+            copy.wait_send()
+        sent.clear()
 
     pl.semaphore_wait(barrier, len(greeted))
     shard_copy.wait()
@@ -485,28 +554,13 @@
     acts_copy.wait()
     prepare_hidden()
     no_halo()
-    kernel_term(1, 0)
-    kernel_term(1, 1)
-    kernel_term(1, 2)
-    reduce_pair("p1", 9, 9)
-    fill_near()
-    near_term(0)
-    near_term(1)
-    mine.wait()
-    gather_1(1)
-    gather_1(2)
-    gather_1(0)
-    near_term(2)
-    fill_far()
-    far_term(0)
-    far_term(1)
-    far_term(2)
+    all_terms()
     reduce_1(1)
-    reduce_1(0)
-    reduce_1(2)
     gather_2(2)
     gather_2(1)
     gather_2(0)
+    reduce_1(0)
+    reduce_1(2)
     reduce_1b(1)
     reduce_1b(0)
     reduce_1b(2)
@@ -539,19 +593,23 @@
     forward_edges(0)
     forward_edges(1)
     forward_edges(2)
-    send_edges()
     reduce_6(1)
     reduce_6(0)
     reduce_6(2)
+    send_edges()
+    forward_inner(0)
     back_edges(0)
+    forward_inner(1)
     back_edges(1)
+    forward_inner(2)
     back_edges(2)
     gather_6(1)
     forward_and_back(0)
     forward_and_back(1)
+    reduce_7(1.0 / lax.axis_size("fsdp"))
     forward_and_back(2)
     write_grad_input()
-    reduce_7(1.0 / lax.axis_size("fsdp"))
+    drain()
     write_outputs()
     reduce_8()
     finish()

time: 64.5 us -> 60.7 us (0.941)
  Pallas kernels: 63.8 us -> 60 us
    pallas_call x1, Pallas kernels: 62.8 us -> 59 us  [body(): pl.pallas_call(step_kernel, out_shape=results, in_specs=[pl.BlockSpec(mem...]
where the time goes in v4:
time: 60.7 us; the launch traced here: 60.6 us
  Pallas kernels  60 us (99%)
  between operations  0.64 us (1%)
    pallas_call x1, Pallas kernels, body(): pl.pallas_call(step_kernel, out_shape=results, in_specs=[pl.BlockSpec(mem...  59 us

profile of v4, /device:TPU:3, one launch (start us, length us, event | category | flops | bytes accessed | tf_op | source)
XLA Modules:
  0.0 60.6 jit_solution(6111651076292621628)
XLA Ops:
  0.6 59.0 %shard_map.58 = (bf16[2,16,16,256]{3,2,1,0:T(8,128)(2,1)S(1)}, bf16[2,16,16,512]{3,2,1,0:T(8,128)(2,1)S(1)}, f32[27,8,256]{2,1,0:T(8,128)S(1)}) custom-call(bf16[2,16,16,512]{3,2,1,0:T(8,128)(2,1)} %bitcast.6, bf16[2,16,16,256]{3,2,1,0:T(8,128)(2,1)} %bitcast.8, bf16[27,8,256]{2,1,0:T(8,128)(2,1)} %bitcast.11), custom_call_target="tpu_custom_call" | custom-call | flops 11000000512 | bytes 4000000 | tf_op jit(solution)/shard_map/pallas_call | solution.py:636
  59.6 1.0 %shard_map.59 = (bf16[2,16,16,256]{3,2,1,0:T(8,128)(2,1)}, bf16[2,16,16,512]{3,2,1,0:T(8,128)(2,1)}, f32[27,8,256]{2,1,0:T(8,128)}) custom-call(bf16[2,16,16,256]{3,2,1,0:T(8,128)(2,1)S(1)} %get-tuple-element.9.outputs, bf16[2,16,16,512]{3,2,1,0:T(8,128)(2,1)S(1)} %get-tuple-element.10.grad_input, f32[27,8,256]{2,1,0:T(8,128)S(1)} %get-tuple-element.11.grad_kernel), custom_call_target="tpu_custom_call" | custom-call | tf_op jit(solution)/shard_map/pallas_call | solution.py:677

commit v5 on v4

--- a/solution.py
+++ b/solution.py
@@ -376,14 +376,17 @@
 
     def kernel_term(colour, b):
         rows = [cot_rows(colour, b, number) for number in range(3)]
-        product = jnp.dot(
-            hidden_t[...], jnp.concatenate(rows, axis=1), preferred_element_type=F32
-        )
-        for number in range(3):
-            for half in range(2):
-                start = 256 * number + 128 * half
-                part = product[:, start : start + 128].reshape(4, 4, 4, 8, 128)
-                partial[half, 9 * colour + 3 * b + number] = part.astype(BF16)
+        rows = jnp.concatenate(rows, axis=1)
+        for top in range(2):
+            product = jnp.dot(
+                hidden_t[256 * top : 256 * top + 256], rows, preferred_element_type=F32
+            )
+            for number in range(3):
+                for half in range(2):
+                    start = 256 * number + 128 * half
+                    part = product[:, start : start + 128].reshape(2, 4, 4, 8, 128)
+                    there = (half, 9 * colour + 3 * b + number, pl.ds(2 * top, 2))
+                    partial[there] = part.astype(BF16)
 
     def tap_weight(tap):
         halves = [weights[half, tap].reshape(512, 128) for half in range(2)]

time: 60.7 us -> 60.7 us (level)
  no operation moved by 1% of the time
where the time goes in v5:
time: 60.7 us; the launch traced here: 60.6 us
  Pallas kernels  60 us (99%)
  between operations  0.64 us (1%)
    pallas_call x1, Pallas kernels, body(): pl.pallas_call(step_kernel, out_shape=results, in_specs=[pl.BlockSpec(mem...  59 us

profile of v5, /device:TPU:3, one launch (start us, length us, event | category | flops | bytes accessed | tf_op | source)
XLA Modules:
  0.0 60.6 jit_solution(8603152017879426584)
XLA Ops:
  0.6 59.0 %shard_map.58 = (bf16[2,16,16,256]{3,2,1,0:T(8,128)(2,1)S(1)}, bf16[2,16,16,512]{3,2,1,0:T(8,128)(2,1)S(1)}, f32[27,8,256]{2,1,0:T(8,128)S(1)}) custom-call(bf16[2,16,16,512]{3,2,1,0:T(8,128)(2,1)} %bitcast.6, bf16[2,16,16,256]{3,2,1,0:T(8,128)(2,1)} %bitcast.8, bf16[27,8,256]{2,1,0:T(8,128)(2,1)} %bitcast.11), custom_call_target="tpu_custom_call" | custom-call | flops 11000000512 | bytes 4000000 | tf_op jit(solution)/shard_map/pallas_call | solution.py:639
  59.6 1.0 %shard_map.59 = (bf16[2,16,16,256]{3,2,1,0:T(8,128)(2,1)}, bf16[2,16,16,512]{3,2,1,0:T(8,128)(2,1)}, f32[27,8,256]{2,1,0:T(8,128)}) custom-call(bf16[2,16,16,256]{3,2,1,0:T(8,128)(2,1)S(1)} %get-tuple-element.9.outputs, bf16[2,16,16,512]{3,2,1,0:T(8,128)(2,1)S(1)} %get-tuple-element.10.grad_input, f32[27,8,256]{2,1,0:T(8,128)S(1)} %get-tuple-element.11.grad_kernel), custom_call_target="tpu_custom_call" | custom-call | tf_op jit(solution)/shard_map/pallas_call | solution.py:680
